TPU v7x, 32 devices: a whole 2x2x4 slice. The times are simulated.
32 devices in a mesh: group: 2 (over x), vocab: 16 (over z, y, core).
Axes of the slice: x: 2, y: 2, z: 4, core: 2. Of those that a mesh axis runs over, the one named last changes fastest.
Arguments:
- shard_ids: int32 [4096, 1], P(('group', 'vocab')), may hold values from 0 to 15; in each aligned block of 128 rows (0 to 127, 128 to 255, ...) at most 16 rows name the same one
- row_ids: int32 [4096], P(('group', 'vocab')), may hold values from 0 to 4007
- table: bfloat16 [64128, 4096], P('vocab', 'group'), may hold values from -6 to 6
- cotangent: bfloat16 [4096, 4096], P(('group', 'vocab')), may hold values from -6 to 6
Outputs:
- embeds: bfloat16 [4096, 4096], P(('group', 'vocab'))
- table_grad: bfloat16 [64128, 4096], P('vocab', 'group')
Inputs may be any that keep to these rules, and one draw needn't show every extreme that they name: `shard_ids`: in each aligned block of 128 rows (the rows of one device), no shard is named by more than 16 rows, and in some blocks one shard is named by exactly 16.
All inputs are finite; a program needn't handle non-finite values.
Results may differ from a plain program's by a relative error of at most 0.001.
Values may be sent and summed in bfloat16 or wider, within the bound.
A program may use at most 128 MiB of HBM per device.

v0:
```python
import jax
import jax.numpy as jnp
from jax import lax
from jax.sharding import PartitionSpec as P


def per_device(shard_ids, row_ids, table, cotangent):
    tokens = cotangent.shape[0]
    width = cotangent.shape[1]
    owners = lax.axis_size("vocab")
    per_owner = 2 * tokens // owners
    slots = owners * per_owner
    rows_here = table.shape[0]
    shard = shard_ids[:, 0]
    owner_hot = (shard[:, None] == jnp.arange(owners, dtype=jnp.int32)[None, :]).astype(jnp.int32)
    ranking = jnp.sum(jnp.cumsum(owner_hot, axis=0) * owner_hot, axis=1) - 1
    slot_index = shard * per_owner + ranking
    slot_hot = slot_index[:, None] == jnp.arange(slots, dtype=jnp.int32)[None, :]
    outgoing = jnp.sum(jnp.where(slot_hot, (row_ids + 1)[:, None], 0), axis=0) - 1
    id_table = lax.all_gather(outgoing.reshape(1, owners, per_owner), "group", axis=0, tiled=True)
    received = lax.all_to_all(id_table, "vocab", split_axis=1, concat_axis=1, tiled=True)
    count = received.shape[0]
    flat = received.reshape(-1)
    picker = (flat[:, None] == jnp.arange(rows_here, dtype=jnp.int32)[None, :]).astype(jnp.bfloat16)
    found = jnp.dot(picker, table, preferred_element_type=jnp.float32).astype(jnp.bfloat16)
    found, picker = (
        found.reshape(received.shape + (table.shape[1],)),
        picker.reshape(count, -1, rows_here),
    )
    homed = lax.all_to_all(found, "vocab", split_axis=1, concat_axis=1, tiled=True)
    joined = lax.all_to_all(homed, "group", split_axis=0, concat_axis=3, tiled=True)
    buffer = joined.reshape(slots, width)
    embeds = jnp.take(buffer, slot_index, axis=0)
    slot_mask = slot_hot.astype(jnp.bfloat16)
    placed = lax.dot_general(
        slot_mask, cotangent, (((0,), (0,)), ((), ())), preferred_element_type=jnp.float32
    )
    sectioned = placed.astype(jnp.bfloat16).reshape(1, owners, per_owner, width)
    owned = lax.all_to_all(sectioned, "vocab", split_axis=1, concat_axis=1, tiled=True)
    arrived = lax.all_to_all(owned, "group", split_axis=3, concat_axis=0, tiled=True)
    flat_grads = arrived.reshape(-1, arrived.shape[3])
    flat_picker = picker.reshape(-1, rows_here)
    table_grad = lax.dot_general(
        flat_picker, flat_grads, (((0,), (0,)), ((), ())), preferred_element_type=jnp.float32
    )
    return (embeds, table_grad.astype(jnp.bfloat16))


def solution(mesh):
    in_specs = (
        P(("group", "vocab"), None),
        P(("group", "vocab")),
        P("vocab", "group"),
        P(("group", "vocab"), None),
    )
    out_specs = (P(("group", "vocab"), None), P("vocab", "group"))
    return jax.shard_map(
        per_device, mesh=mesh, in_specs=in_specs, out_specs=out_specs, check_vma=False
    )
```

profile of v0, /device:TPU:14, one launch (start us, length us, event | category | flops | bytes accessed | tf_op | source)
XLA Modules:
  0.0 217.1 jit_solution(9947631691432889317)
XLA Ops:
  0.6 0.0 copy-start
  0.6 0.7 broadcast_add_fusion.1
  1.4 0.7 fusion.5
  2.1 0.2 reduce_window_sum.11
  2.3 0.8 select_reduce_fusion.1
  3.1 0.7 and_bitcast_fusion
  3.8 0.1 select_reduce_fusion
  3.9 0.1 sub.14
  4.0 4.4 %all_gather.3 = s32[2,16,16]{2,1,0:T(8,128)S(1)} all-gather(s32[1,16,16]{2,1,0:T(8,128)S(1)} %sub.14), channel_id=1, replica_groups=mesh['group'=2,'vocab'=16] {'group'}, dimensions={0}, use_global_device_ids=true | all-gather | bytes 3072 | tf_op jit(solution)/shard_map/all_gather | solution.py:20
  8.4 0.6 copy.34
  9.0 6.2 %all-to-all-start = ((s32[2,16,16]{2,0,1:T(2,128)}), s32[2,16,16]{2,0,1:T(2,128)S(1)}, u32[]{:S(2)}, u32[]{:S(2)}) async-start(s32[2,16,16]{2,0,1:T(2,128)} %copy.34), calls=%async_computation | async-start | bytes 32768 | tf_op jit(solution)/shard_map/all_to_all | solution.py:21
  15.2 0.0 copy-done
  15.2 2.1 convolution_convert_fusion.1
  17.4 2.0 all-to-all-done
  19.4 6.0 %all-to-all-start.3 = ((bf16[1,16,16,4096]{3,2,0,1:T(8,128)(2,1)}), bf16[1,16,16,4096]{3,2,0,1:T(8,128)(2,1)S(1)}, u32[]{:S(2)}, u32[]{:S(2)}) async-start(bf16[1,16,16,4096]{3,2,0,1:T(8,128)(2,1)} %bitcast.31), calls=%async_computation.3 | async-start | bytes 4194304 | tf_op jit(solution)/shard_map/all_to_all | solution.py:39
  25.4 0.1 eq.53
  25.4 12.5 %fusion.3 = bf16[512,2048]{1,0:T(8,128)(2,1)S(1)} fusion(bf16[4008,2048]{1,0:T(8,128)(2,1)} %param.6, s32[512]{0:T(512)S(1)} %eq.53), kind=kOutput, calls=%fused_computation.7 | convolution fusion | flops 8408485888 | bytes 18515968 | tf_op jit(solution)/shard_map/dot_general | solution.py:25
  37.9 1.5 copy.36
  39.4 33.1 %all-to-all-done.3 = bf16[1,16,16,4096]{3,2,0,1:T(8,128)(2,1)S(1)} async-done(((bf16[1,16,16,4096]{3,2,0,1:T(8,128)(2,1)}), bf16[1,16,16,4096]{3,2,0,1:T(8,128)(2,1)S(1)}, u32[]{:S(2)}, u32[]{:S(2)}) %all-to-all-start.3) | async-done | bytes 2097184 | tf_op jit(solution)/shard_map/all_to_all | solution.py:39
  72.5 5.0 %all-to-all-start.1 = ((bf16[2,16,16,2048]{3,2,0,1:T(8,128)(2,1)}), bf16[2,16,16,2048]{3,2,0,1:T(8,128)(2,1)}, u32[]{:S(2)}, u32[]{:S(2)}) async-start(bf16[2,16,16,2048]{3,2,0,1:T(8,128)(2,1)} %copy.36), calls=%async_computation.1 | async-start | bytes 4194304 | tf_op jit(solution)/shard_map/all_to_all | solution.py:30
  77.6 14.0 %copy.40 = bf16[1,16,16,4096]{2,1,0,3:T(8,128)(2,1)} copy(bf16[1,16,16,4096]{3,2,0,1:T(8,128)(2,1)S(1)} %all-to-all-done.3) | data formatting | bytes 4194304 | tf_op jit(solution)/shard_map/all_to_all | solution.py:39
  91.6 26.0 %reshape.60 = bf16[2,2,262144]{2,1,0:T(2,128)(2,1)} reshape(bf16[4096,1,16,16]{3,2,1,0:T(8,128)(2,1)} %bitcast.27) | data formatting | bytes 4194304
  117.6 7.2 %all-to-all-done.1 = bf16[2,16,16,2048]{3,2,0,1:T(8,128)(2,1)} async-done(((bf16[2,16,16,2048]{3,2,0,1:T(8,128)(2,1)}), bf16[2,16,16,2048]{3,2,0,1:T(8,128)(2,1)}, u32[]{:S(2)}, u32[]{:S(2)}) %all-to-all-start.1) | async-done | bytes 2097184 | tf_op jit(solution)/shard_map/all_to_all | solution.py:30
  124.8 4.3 %all-to-all-start.4 = ((bf16[2,2,262144]{2,1,0:T(2,128)(2,1)}), bf16[2,2,262144]{2,1,0:T(2,128)(2,1)S(1)}, u32[]{:S(2)}, u32[]{:S(2)}) async-start(bf16[2,2,262144]{2,1,0:T(2,128)(2,1)} %reshape.60), calls=%async_computation.4 | async-start | bytes 4194304 | tf_op jit(solution)/shard_map/all_to_all | solution.py:40
  129.1 3.2 %copy.37 = bf16[2,16,16,2048]{3,2,1,0:T(8,128)(2,1)} copy(bf16[2,16,16,2048]{3,2,0,1:T(8,128)(2,1)} %all-to-all-done.1) | data formatting | bytes 4194304 | tf_op jit(solution)/shard_map/all_to_all | solution.py:30
  132.3 20.8 %all-to-all-done.4 = bf16[2,2,262144]{2,1,0:T(2,128)(2,1)S(1)} async-done(((bf16[2,2,262144]{2,1,0:T(2,128)(2,1)}), bf16[2,2,262144]{2,1,0:T(2,128)(2,1)S(1)}, u32[]{:S(2)}, u32[]{:S(2)}) %all-to-all-start.4) | async-done | bytes 2097184 | tf_op jit(solution)/shard_map/all_to_all | solution.py:40
  153.0 6.6 %all-to-all-start.2 = ((bf16[2,16,16,2048]{3,2,1,0:T(8,128)(2,1)}), bf16[2,16,16,2048]{3,2,1,0:T(8,128)(2,1)}, u32[]{:S(2)}, u32[]{:S(2)}) async-start(bf16[2,16,16,2048]{3,2,1,0:T(8,128)(2,1)} %copy.37), calls=%async_computation.2 | async-start | bytes 4194304 | tf_op jit(solution)/shard_map/all_to_all | solution.py:31
  159.6 17.7 %reshape.61 = bf16[4096,1,16,16]{3,2,1,0:T(8,128)(2,1)} reshape(bf16[2,2,262144]{2,1,0:T(2,128)(2,1)S(1)} %all-to-all-done.4) | data formatting | bytes 4194304
  177.2 17.3 %copy.43 = bf16[1,16,16,2,2048]{4,3,2,1,0:T(2,128)(2,1)S(1)} copy(bf16[1,16,16,2,2048]{2,1,4,3,0:T(8,128)(2,1)} %bitcast.28) | data formatting | bytes 4194304 | tf_op jit(solution)/shard_map/all_to_all | solution.py:40
  194.5 0.9 copy.42
  195.4 12.4 %convolution_convert_fusion = bf16[4008,2048]{1,0:T(8,128)(2,1)} fusion(bf16[512,2048]{1,0:T(8,128)(2,1)S(1)} %bitcast.33, s32[512]{0:T(512)S(1)} %eq.53), kind=kOutput, calls=%fused_computation.1 | convolution fusion | flops 8415645696 | bytes 18515968 | tf_op jit(solution)/shard_map/dot_general | solution.py:43
  207.9 0.0 all-to-all-done.2
  207.9 3.8 %copy.38 = bf16[1,16,16,2,2048]{4,3,2,1,0:T(2,128)(2,1)S(1)} copy(bf16[1,16,16,2,2048]{4,2,1,3,0:T(8,128)(2,1)} %bitcast.6) | data formatting | bytes 4194304 | tf_op jit(solution)/shard_map/all_to_all | solution.py:31
  211.7 0.9 copy.44
  212.6 0.0 copy-start.1
  212.6 2.2 gather_fusion
  214.7 2.4 %broadcast_select_fusion = bf16[128,4096]{1,0:T(8,128)(2,1)} fusion(bf16[128,4096]{1,0:T(8,128)(2,1)} %gather_fusion, pred[128]{0:T(512)(128)(4,1)S(1)} %get-tuple-element.2), kind=kLoop, calls=%fused_computation.8 | loop fusion | flops 524288 | bytes 2097280 | tf_op jit(solution)/shard_map/jit(_take)/select_n | solution.py:33
  217.1 0.0 copy-done.1
  (4 shorter events, 0.0 us)
Async XLA Ops:
  0.6 14.6 %copy-start = (bf16[128,4096]{1,0:T(8,128)(2,1)S(1)}, bf16[128,4096]{1,0:T(8,128)(2,1)}, u32[]{:S(2)}) copy-start(bf16[128,4096]{1,0:T(8,128)(2,1)} %param.7) | copy-start | bytes 3145732
  9.0 10.4 %all-to-all-start = ((s32[2,16,16]{2,0,1:T(2,128)}), s32[2,16,16]{2,0,1:T(2,128)S(1)}, u32[]{:S(2)}, u32[]{:S(2)}) async-start(s32[2,16,16]{2,0,1:T(2,128)} %copy.34), calls=%async_computation | async-start | bytes 32768 | tf_op jit(solution)/shard_map/all_to_all | solution.py:21
  19.4 53.2 %all-to-all-start.3 = ((bf16[1,16,16,4096]{3,2,0,1:T(8,128)(2,1)}), bf16[1,16,16,4096]{3,2,0,1:T(8,128)(2,1)S(1)}, u32[]{:S(2)}, u32[]{:S(2)}) async-start(bf16[1,16,16,4096]{3,2,0,1:T(8,128)(2,1)} %bitcast.31), calls=%async_computation.3 | async-start | bytes 4194304 | tf_op jit(solution)/shard_map/all_to_all | solution.py:39
  72.5 52.3 %all-to-all-start.1 = ((bf16[2,16,16,2048]{3,2,0,1:T(8,128)(2,1)}), bf16[2,16,16,2048]{3,2,0,1:T(8,128)(2,1)}, u32[]{:S(2)}, u32[]{:S(2)}) async-start(bf16[2,16,16,2048]{3,2,0,1:T(8,128)(2,1)} %copy.36), calls=%async_computation.1 | async-start | bytes 4194304 | tf_op jit(solution)/shard_map/all_to_all | solution.py:30
  124.8 28.2 %all-to-all-start.4 = ((bf16[2,2,262144]{2,1,0:T(2,128)(2,1)}), bf16[2,2,262144]{2,1,0:T(2,128)(2,1)S(1)}, u32[]{:S(2)}, u32[]{:S(2)}) async-start(bf16[2,2,262144]{2,1,0:T(2,128)(2,1)} %reshape.60), calls=%async_computation.4 | async-start | bytes 4194304 | tf_op jit(solution)/shard_map/all_to_all | solution.py:40
  153.0 54.8 %all-to-all-start.2 = ((bf16[2,16,16,2048]{3,2,1,0:T(8,128)(2,1)}), bf16[2,16,16,2048]{3,2,1,0:T(8,128)(2,1)}, u32[]{:S(2)}, u32[]{:S(2)}) async-start(bf16[2,16,16,2048]{3,2,1,0:T(8,128)(2,1)} %copy.37), calls=%async_computation.2 | async-start | bytes 4194304 | tf_op jit(solution)/shard_map/all_to_all | solution.py:31
  212.6 4.5 %copy-start.1 = (bf16[128,4096]{1,0:T(8,128)(2,1)S(1)}, bf16[128,4096]{1,0:T(8,128)(2,1)}, u32[]{:S(2)}) copy-start(bf16[128,4096]{1,0:T(8,128)(2,1)} %param.7) | copy-start | bytes 3145732
where the time goes:
time: 218 us; the launch traced here: 217 us
  local copies, waits for them, and re-layouts  88.1 us (40%)
  waiting for transfers between devices  63.1 us (29%)
  starting transfers between devices  28.1 us (13%)
  matrix products  27.1 us (12%)
  other arithmetic  5.63 us (3%)
  blocking collectives  4.36 us (2%)
    unnamed x7, local copies, waits for them, and re-layouts  44.6 us
    all_to_all x1, waiting for transfers between devices, per_device(): lax.all_to_all(sectioned, 'vocab', split_axis=1, concat_axis=1, tiled=True)  33.1 us
    all_to_all x1, waiting for transfers between devices, per_device(): lax.all_to_all(owned, 'group', split_axis=3, concat_axis=0, tiled=True)  20.8 us
    all_to_all x2, local copies, waits for them, and re-layouts, per_device(): lax.all_to_all(owned, 'group', split_axis=3, concat_axis=0, tiled=True)  18.2 us
    all_to_all x1, local copies, waits for them, and re-layouts, per_device(): lax.all_to_all(sectioned, 'vocab', split_axis=1, concat_axis=1, tiled=True)  14 us
    dot_general x1, matrix products, per_device(): jnp.dot(picker, table, preferred_element_type=jnp.float32)  12.5 us
    dot_general x1, matrix products, per_device(): lax.dot_general(flat_picker, flat_grads, (((0,), (0,)), ((), ())), prefer...  12.4 us
    all_to_all x1, waiting for transfers between devices, per_device(): lax.all_to_all(found, 'vocab', split_axis=1, concat_axis=1, tiled=True)  7.21 us
  transfers between devices with their start and end apart: 5, of which 4 were waited for; matrix products, arithmetic and copies ran while one was open for 50% of the time, Pallas kernels for 0%

commit v1 on v0

v1 whole, which is shorter than its diff:
```python
import jax
import jax.numpy as jnp
from jax import lax
from jax.sharding import PartitionSpec as P

BOTH = ("group", "vocab")


def per_device(shard_ids, row_ids, table, cotangent):
    tokens, width = cotangent.shape
    groups = lax.axis_size("group")
    owners = lax.axis_size("vocab")
    per_owner = 2 * tokens // owners
    slots = owners * per_owner
    rows_here, cols = table.shape
    shard = shard_ids[:, 0]
    owner_hot = (shard[:, None] == jnp.arange(owners, dtype=jnp.int32)[None, :]).astype(jnp.bfloat16)
    earlier = jnp.tril(jnp.ones((tokens, tokens), jnp.bfloat16), -1)
    before = jnp.dot(earlier, owner_hot, preferred_element_type=jnp.float32)
    ranking = jnp.sum(before * owner_hot.astype(jnp.float32), axis=1).astype(jnp.int32)
    slot_index = shard * per_owner + ranking
    slot_hot = slot_index[:, None] == jnp.arange(slots, dtype=jnp.int32)[None, :]
    slot_mask = slot_hot.astype(jnp.bfloat16)
    outgoing = jnp.sum(jnp.where(slot_hot, (row_ids + 1)[:, None], 0), axis=0) - 1

    placed = jnp.concatenate(
        [
            lax.dot_general(
                slot_mask,
                cotangent[:, g * cols : (g + 1) * cols],
                (((0,), (0,)), ((), ())),
                preferred_element_type=jnp.float32,
            ).astype(jnp.bfloat16)
            for g in range(groups)
        ],
        axis=0,
    )
    arrived = lax.all_to_all(placed, BOTH, split_axis=0, concat_axis=0, tiled=True)

    asked = jnp.concatenate([outgoing] * groups)
    received = lax.all_to_all(asked, BOTH, split_axis=0, concat_axis=0, tiled=True)
    picker = (received[:, None] == jnp.arange(rows_here, dtype=jnp.int32)[None, :]).astype(jnp.bfloat16)
    found = jnp.dot(picker, table, preferred_element_type=jnp.float32).astype(jnp.bfloat16)
    homed = lax.all_to_all(found, BOTH, split_axis=0, concat_axis=0, tiled=True)

    table_grad = lax.dot_general(
        picker, arrived, (((0,), (0,)), ((), ())), preferred_element_type=jnp.float32
    ).astype(jnp.bfloat16)
    embeds = jnp.concatenate(
        [
            jnp.dot(
                slot_mask, homed[g * slots : (g + 1) * slots], preferred_element_type=jnp.float32
            ).astype(jnp.bfloat16)
            for g in range(groups)
        ],
        axis=1,
    )
    return embeds, table_grad


def solution(mesh):
    in_specs = (
        P(BOTH, None),
        P(BOTH),
        P("vocab", "group"),
        P(BOTH, None),
    )
    out_specs = (P(BOTH, None), P("vocab", "group"))
    return jax.shard_map(
        per_device, mesh=mesh, in_specs=in_specs, out_specs=out_specs, check_vma=False
    )
```

time: 218 us -> 128 us (0.59)
  the two profiles are of different devices: /device:TPU:14 before, /device:TPU:0 now
where the time goes in v1:
time: 128 us
  waiting for transfers between devices  73.6 us (57%)
  matrix products  32.4 us (25%)
  starting transfers between devices  13.5 us (11%)
  other arithmetic  5.41 us (4%)
  local copies, waits for them, and re-layouts  2.2 us (2%)
    all_to_all x1, waiting for transfers between devices, per_device(): homed = lax.all_to_all(found, BOTH, split_axis=0, concat_axis=0, tiled=True)  36 us
    all_to_all x1, waiting for transfers between devices, per_device(): lax.all_to_all(placed, BOTH, split_axis=0, concat_axis=0, tiled=True)  35.3 us
    dot_general x1, matrix products, per_device(): lax.dot_general(picker, arrived, (((0,), (0,)), ((), ())), preferred_elem...  14.1 us
    dot_general x1, matrix products, per_device(): jnp.dot(picker, table, preferred_element_type=jnp.float32)  13.5 us
    all_to_all x1, starting transfers between devices, per_device(): lax.all_to_all(asked, BOTH, split_axis=0, concat_axis=0, tiled=True)  7.33 us
    all_to_all x1, starting transfers between devices, per_device(): lax.all_to_all(placed, BOTH, split_axis=0, concat_axis=0, tiled=True)  3.49 us
    dot_general x2, matrix products, per_device(): lax.dot_general(slot_mask, cotangent[:, g * cols:(g + 1) * cols], (((0,),...  3.18 us
    all_to_all x1, starting transfers between devices, per_device(): homed = lax.all_to_all(found, BOTH, split_axis=0, concat_axis=0, tiled=True)  2.73 us
  transfers between devices with their start and end apart: 3, of which 3 were waited for; matrix products, arithmetic and copies ran while one was open for 26% of the time, Pallas kernels for 0%

profile of v1, /device:TPU:0, one launch (start us, length us, event | category | flops | bytes accessed | tf_op | source)
XLA Modules:
  0.0 127.9 jit_solution(14088774210910284093)
XLA Ops:
  0.6 0.7 broadcast_add_fusion.1
  1.3 0.9 fusion.4
  2.2 0.7 fusion.18
  2.9 0.1 select_reduce_fusion
  3.0 0.1 sub.7
  3.1 0.6 pad_add_fusion
  3.7 7.3 %all-to-all-start = ((s32[32,16,1]{1,2,0:T(1,128)}), s32[32,16,1]{1,2,0:T(1,128)S(1)}, u32[]{:S(2)}, u32[]{:S(2)}) async-start(s32[32,16,1]{1,2,0:T(1,128)} %bitcast.3), calls=%async_computation | async-start | bytes 32768 | tf_op jit(solution)/shard_map/all_to_all | solution.py:41
  11.1 1.6 %convolution_convert_fusion.1 = bf16[256,2048]{1,0:T(8,128)(2,1)S(1)} fusion(bf16[128,4096]{1,0:T(8,128)(2,1)} %param.7, s32[128]{0:T(128)S(1)} %fusion.18), kind=kOutput, calls=%fused_computation.6 | convolution fusion | flops 134774784 | bytes 1573376 | tf_op jit(solution)/shard_map/dot_general | solution.py:28
  12.7 1.6 %convolution_convert_fusion.2 = bf16[256,2048]{1,0:T(8,128)(2,1)S(1)} fusion(bf16[128,4096]{1,0:T(8,128)(2,1)} %param.7, s32[128]{0:T(128)S(1)} %fusion.18), kind=kOutput, calls=%fused_computation.7 | convolution fusion | flops 134774784 | bytes 1573376 | tf_op jit(solution)/shard_map/dot_general | solution.py:28
  14.3 1.6 %pad_maximum_fusion = bf16[512,2048]{1,0:T(8,128)(2,1)} fusion(bf16[256,2048]{1,0:T(8,128)(2,1)S(1)} %convolution_convert_fusion.1, bf16[256,2048]{1,0:T(8,128)(2,1)S(1)} %convolution_convert_fusion.2), kind=kLoop, calls=%fused_computation.10 | loop fusion | flops 4194304 | bytes 4194304 | tf_op jit(solution)/shard_map/concatenate | solution.py:26
  15.8 2.3 %all-to-all-done = s32[32,16,1]{1,2,0:T(1,128)S(1)} async-done(((s32[32,16,1]{1,2,0:T(1,128)}), s32[32,16,1]{1,2,0:T(1,128)S(1)}, u32[]{:S(2)}, u32[]{:S(2)}) %all-to-all-start) | async-done | bytes 2080 | tf_op jit(solution)/shard_map/all_to_all | solution.py:41
  18.2 3.5 %all-to-all-start.2 = ((bf16[32,16,2048]{2,1,0:T(8,128)(2,1)}), bf16[32,16,2048]{2,1,0:T(8,128)(2,1)S(1)}, u32[]{:S(2)}, u32[]{:S(2)}) async-start(bf16[32,16,2048]{2,1,0:T(8,128)(2,1)} %bitcast.7), calls=%async_computation.2 | async-start | bytes 4194304 | tf_op jit(solution)/shard_map/all_to_all | solution.py:38
  21.7 0.5 broadcast.22
  22.2 0.7 reduce.3
  22.9 0.1 eq.53
  23.0 13.5 %fusion.3 = bf16[512,2048]{1,0:T(8,128)(2,1)} fusion(bf16[4008,2048]{1,0:T(8,128)(2,1)} %param.6, s32[512]{0:T(512)S(1)} %eq.53), kind=kOutput, calls=%fused_computation.5 | convolution fusion | flops 8408485888 | bytes 18515968 | tf_op jit(solution)/shard_map/dot_general | solution.py:43
  36.4 35.3 %all-to-all-done.2 = bf16[32,16,2048]{2,1,0:T(8,128)(2,1)S(1)} async-done(((bf16[32,16,2048]{2,1,0:T(8,128)(2,1)}), bf16[32,16,2048]{2,1,0:T(8,128)(2,1)S(1)}, u32[]{:S(2)}, u32[]{:S(2)}) %all-to-all-start.2) | async-done | bytes 2097184 | tf_op jit(solution)/shard_map/all_to_all | solution.py:38
  71.7 0.0 copy-start
  71.7 1.3 %copy-done = bf16[32,16,2048]{2,1,0:T(8,128)(2,1)} copy-done((bf16[32,16,2048]{2,1,0:T(8,128)(2,1)}, bf16[32,16,2048]{2,1,0:T(8,128)(2,1)S(1)}, u32[]{:S(2)}) %copy-start) | copy-done | bytes 2097176
  73.0 2.7 %all-to-all-start.1 = ((bf16[32,16,2048]{2,1,0:T(8,128)(2,1)}), bf16[32,16,2048]{2,1,0:T(8,128)(2,1)S(1)}, u32[]{:S(2)}, u32[]{:S(2)}) async-start(bf16[32,16,2048]{2,1,0:T(8,128)(2,1)} %bitcast.21), calls=%async_computation.1 | async-start | bytes 4194304 | tf_op jit(solution)/shard_map/all_to_all | solution.py:44
  75.8 14.1 %convolution_convert_fusion = bf16[4008,2048]{1,0:T(8,128)(2,1)} fusion(bf16[512,2048]{1,0:T(8,128)(2,1)} %bitcast.20, s32[512]{0:T(512)S(1)} %eq.53), kind=kOutput, calls=%fused_computation | convolution fusion | flops 8415645696 | bytes 18515968 | tf_op jit(solution)/shard_map/dot_general | solution.py:46
  89.9 36.0 %all-to-all-done.1 = bf16[32,16,2048]{2,1,0:T(8,128)(2,1)S(1)} async-done(((bf16[32,16,2048]{2,1,0:T(8,128)(2,1)}), bf16[32,16,2048]{2,1,0:T(8,128)(2,1)S(1)}, u32[]{:S(2)}, u32[]{:S(2)}) %all-to-all-start.1) | async-done | bytes 2097184 | tf_op jit(solution)/shard_map/all_to_all | solution.py:44
  125.9 0.2 fusion.21
  126.1 0.4 convolution_convert_fusion.4
  126.5 0.3 convolution_convert_fusion.3
  126.8 1.1 pad_maximum_fusion.1
  (2 shorter events, 0.0 us)
Async XLA Ops:
  3.7 14.4 %all-to-all-start = ((s32[32,16,1]{1,2,0:T(1,128)}), s32[32,16,1]{1,2,0:T(1,128)S(1)}, u32[]{:S(2)}, u32[]{:S(2)}) async-start(s32[32,16,1]{1,2,0:T(1,128)} %bitcast.3), calls=%async_computation | async-start | bytes 32768 | tf_op jit(solution)/shard_map/all_to_all | solution.py:41
  18.2 53.6 %all-to-all-start.2 = ((bf16[32,16,2048]{2,1,0:T(8,128)(2,1)}), bf16[32,16,2048]{2,1,0:T(8,128)(2,1)S(1)}, u32[]{:S(2)}, u32[]{:S(2)}) async-start(bf16[32,16,2048]{2,1,0:T(8,128)(2,1)} %bitcast.7), calls=%async_computation.2 | async-start | bytes 4194304 | tf_op jit(solution)/shard_map/all_to_all | solution.py:38
  71.7 1.3 %copy-start = (bf16[32,16,2048]{2,1,0:T(8,128)(2,1)}, bf16[32,16,2048]{2,1,0:T(8,128)(2,1)S(1)}, u32[]{:S(2)}) copy-start(bf16[32,16,2048]{2,1,0:T(8,128)(2,1)S(1)} %all-to-all-done.2) | copy-start | bytes 6291460
  73.0 52.9 %all-to-all-start.1 = ((bf16[32,16,2048]{2,1,0:T(8,128)(2,1)}), bf16[32,16,2048]{2,1,0:T(8,128)(2,1)S(1)}, u32[]{:S(2)}, u32[]{:S(2)}) async-start(bf16[32,16,2048]{2,1,0:T(8,128)(2,1)} %bitcast.21), calls=%async_computation.1 | async-start | bytes 4194304 | tf_op jit(solution)/shard_map/all_to_all | solution.py:44
